TPU v7x, 32 devices: a whole 2x2x4 slice. The times are simulated.
32 devices in a mesh: dev: 8 (over z, y), rep: 4 (over x, core).
Axes of the slice: x: 2, y: 2, z: 4, core: 2. Of those that a mesh axis runs over, the one named last changes fastest.
Arguments:
- features: bfloat16 [32768, 256], P(('dev', 'rep')), may hold values from -6 to 6
- history: bfloat16 [32768, 256], P(('dev', 'rep')), may hold values from -6 to 6
- new_owner: int32 [32, 8], P(('dev', 'rep')), may hold values from 0 to 7, as said below
- pull_rows: int32 [32768], P(('dev', 'rep')), may hold values from 0 to 1023
- occupancy: int32 [256, 16], P(('dev', 'rep')), may hold values from 0 to 1, as said below
- adj_local: bfloat16 [32768, 1024], P(('dev', 'rep')), may hold values from -0.125 to 0.125
- adj_boundary: bfloat16 [32768, 1024], P(('dev', 'rep')), may hold values from -0.125 to 0.125
- w_first: bfloat16 [256, 256], replicated, may hold values from -0.375 to 0.375
- bias_first: float32 [256], replicated, may hold values from -3 to 3
- w_second: bfloat16 [256, 256], replicated, may hold values from -0.375 to 0.375
- cotangent: bfloat16 [32768, 256], P(('dev', 'rep')), may hold values from -6 to 6
Outputs:
- hidden: bfloat16 [32768, 256], P(('dev', 'rep'))
- output: bfloat16 [32768, 256], P(('dev', 'rep'))
- w_second_grad: float32 [256, 256], replicated
Inputs may be any that keep to these rules, and one draw needn't show every extreme that they name: Each row of new_owner is a permutation of 0 to 7. `occupancy`: tile flags of 0 or 1.
All inputs are finite; a program needn't handle non-finite values.
Results may differ from a plain program's by a relative error of at most 0.0061.
Values may be sent and summed in bfloat16 or wider, within the bound.
A program may use at most 64 MiB of HBM per device.

v0:
```python
import jax
import jax.numpy as jnp
from jax import lax
from jax.sharding import PartitionSpec as P


def expand(occupied):
    return jnp.repeat(jnp.repeat(occupied, 128, axis=0), 128, axis=1).astype(jnp.bfloat16)


def dense_terms(owned, remote, adj_local, adj_boundary, occupancy):
    height = owned.shape[0]
    full_mask = expand(occupancy)
    local_tile = adj_local * full_mask[:, :height]
    edge_tile = adj_boundary * full_mask[:, height:]
    summed = jnp.dot(local_tile, owned, preferred_element_type=jnp.float32)
    summed = summed + jnp.dot(edge_tile, remote, preferred_element_type=jnp.float32)
    partial_value = lax.dot_general(
        edge_tile, owned, (((0,), (0,)), ((), ())), preferred_element_type=jnp.float32
    )
    return (summed, partial_value)


def body(
    features,
    history,
    new_owner,
    pull_rows,
    occupancy,
    adj_local,
    adj_boundary,
    w_first,
    bias_first,
    w_second,
    cotangent,
):
    peer_count = lax.axis_size("dev")
    height, breadth = features.shape
    cluster = height // peer_count
    pulled = pull_rows.shape[0]
    per_peer = pulled // peer_count
    indices = jnp.arange(peer_count, dtype=jnp.int32)
    matches = (new_owner[0][:, None] == indices[None, :]).astype(jnp.int32)
    inverse = jnp.sum(matches * indices[:, None], axis=0)

    def arrange(values):
        return values.reshape(peer_count, cluster, breadth)[inverse]

    requests = lax.all_to_all(
        pull_rows.reshape(peer_count, per_peer), "dev", split_axis=0, concat_axis=0, tiled=True
    ).reshape(pulled)

    def fetch_rows(values):
        return values[requests].reshape(peer_count, per_peer, breadth)

    selector = (requests[None, :] == jnp.arange(height, dtype=jnp.int32)[:, None]).astype(
        jnp.bfloat16
    )

    def collect(received):
        return jnp.dot(
            selector, received.reshape(pulled, breadth), preferred_element_type=jnp.float32
        )

    def layer_terms(owned, remote):
        return dense_terms(owned, remote, adj_local, adj_boundary, occupancy)

    moved_x, moved_h = (
        lax.all_to_all(arrange(features), "dev", split_axis=0, concat_axis=0, tiled=True),
        lax.all_to_all(arrange(history), "dev", split_axis=0, concat_axis=0, tiled=True),
    )
    own_x = moved_x.reshape(height, breadth)
    own_h = moved_h.reshape(height, breadth)
    far_x, far_h = (
        lax.all_to_all(fetch_rows(own_x), "dev", split_axis=0, concat_axis=0, tiled=True),
        lax.all_to_all(fetch_rows(own_h), "dev", split_axis=0, concat_axis=0, tiled=True),
    )
    summed_one, partial_one = layer_terms(own_x, far_x.reshape(pulled, breadth))
    pushed_one = lax.all_to_all(
        partial_one.astype(jnp.bfloat16).reshape(peer_count, per_peer, breadth),
        "dev",
        split_axis=0,
        concat_axis=0,
        tiled=True,
    )
    far_h = far_h.reshape(pulled, breadth)
    aggregate_one = (summed_one + collect(pushed_one)).astype(jnp.bfloat16)
    hidden = jnp.maximum(
        jnp.dot(aggregate_one, w_first, preferred_element_type=jnp.float32) + bias_first, 0.0
    ).astype(jnp.bfloat16)
    summed_two, partial_two = layer_terms(hidden, far_h)
    pushed_two = lax.all_to_all(
        partial_two.astype(jnp.bfloat16).reshape(peer_count, per_peer, breadth),
        "dev",
        split_axis=0,
        concat_axis=0,
        tiled=True,
    )
    aggregate_two = (summed_two + collect(pushed_two)).astype(jnp.bfloat16)
    output = jnp.dot(aggregate_two, w_second, preferred_element_type=jnp.float32).astype(
        jnp.bfloat16
    )
    local_grad = lax.dot_general(
        aggregate_two, cotangent, (((0,), (0,)), ((), ())), preferred_element_type=jnp.float32
    )
    gradient = lax.psum(local_grad, ("dev", "rep"))
    return (hidden, output, gradient)


def solution(mesh):
    return jax.shard_map(
        body,
        mesh=mesh,
        in_specs=(
            P(("dev", "rep"), None),
            P(("dev", "rep"), None),
            P(("dev", "rep"), None),
            P(("dev", "rep")),
            P(("dev", "rep"), None),
            P(("dev", "rep"), None),
            P(("dev", "rep"), None),
            P(),
            P(),
            P(),
            P(("dev", "rep"), None),
        ),
        out_specs=(P(("dev", "rep"), None), P(("dev", "rep"), None), P()),
        check_vma=False,
    )
```

profile of v0, /device:TPU:0, one launch (start us, length us, event | category | flops | bytes accessed | tf_op | source)
XLA Modules:
  0.0 263.3 jit_solution(17940252568643423680)
XLA Ops:
  7.2 7.5 %all-to-all-start.1 = ((s32[8,1,128]{2,1,0:T(1,128)}), s32[8,1,128]{2,1,0:T(1,128)S(1)}, u32[]{:S(2)}, u32[]{:S(2)}) async-start(s32[8,1,128]{2,1,0:T(1,128)} %bitcast.62), calls=%async_computation.1 | async-start | bytes 8192 | tf_op jit(solution)/shard_map/all_to_all | solution.py:49
  16.8 4.3 %all-to-all-done.1 = s32[8,1,128]{2,1,0:T(1,128)S(1)} async-done(((s32[8,1,128]{2,1,0:T(1,128)}), s32[8,1,128]{2,1,0:T(1,128)S(1)}, u32[]{:S(2)}, u32[]{:S(2)}) %all-to-all-start.1) | async-done | bytes 4128 | tf_op jit(solution)/shard_map/all_to_all | solution.py:49
  21.1 3.5 %all-to-all-start = ((bf16[8,128,256]{2,1,0:T(8,128)(2,1)}), bf16[8,128,256]{2,1,0:T(8,128)(2,1)S(1)}, u32[]{:S(2)}, u32[]{:S(2)}) async-start(bf16[8,128,256]{2,1,0:T(8,128)(2,1)} %gather_fusion), calls=%async_computation | async-start | bytes 1048576 | tf_op jit(solution)/shard_map/all_to_all | solution.py:69
  25.9 11.9 %all-to-all-done = bf16[8,128,256]{2,1,0:T(8,128)(2,1)S(1)} async-done(((bf16[8,128,256]{2,1,0:T(8,128)(2,1)}), bf16[8,128,256]{2,1,0:T(8,128)(2,1)S(1)}, u32[]{:S(2)}, u32[]{:S(2)}) %all-to-all-start) | async-done | bytes 524320 | tf_op jit(solution)/shard_map/all_to_all | solution.py:69
  37.8 3.7 %all-to-all-start.4 = ((bf16[8,128,256]{2,1,0:T(8,128)(2,1)}), bf16[8,128,256]{2,1,0:T(8,128)(2,1)S(1)}, u32[]{:S(2)}, u32[]{:S(2)}) async-start(bf16[8,128,256]{2,1,0:T(8,128)(2,1)} %gather_fusion.2), calls=%async_computation.4 | async-start | bytes 1048576 | tf_op jit(solution)/shard_map/all_to_all | solution.py:70
  41.5 5.0 %gather_fusion.1 = bf16[1024,256]{1,0:T(8,128)(2,1)} fusion(bf16[1024,256]{1,0:T(8,128)(2,1)S(1)} %bitcast.45, s32[1024]{0:T(1024)S(1)} %broadcast_clamp_fusion), kind=kCustom, calls=%fused_computation.1 | custom fusion | bytes 1052672 | tf_op jit(solution)/shard_map/gather | solution.py:54
  46.5 8.8 %all-to-all-done.4 = bf16[8,128,256]{2,1,0:T(8,128)(2,1)S(1)} async-done(((bf16[8,128,256]{2,1,0:T(8,128)(2,1)}), bf16[8,128,256]{2,1,0:T(8,128)(2,1)S(1)}, u32[]{:S(2)}, u32[]{:S(2)}) %all-to-all-start.4) | async-done | bytes 524320 | tf_op jit(solution)/shard_map/all_to_all | solution.py:70
  55.3 4.2 %all-to-all-start.2 = ((bf16[8,128,256]{2,1,0:T(8,128)(2,1)}), bf16[8,128,256]{2,1,0:T(8,128)(2,1)}, u32[]{:S(2)}, u32[]{:S(2)}) async-start(bf16[8,128,256]{2,1,0:T(8,128)(2,1)} %bitcast.9), calls=%async_computation.2 | async-start | bytes 1048576 | tf_op jit(solution)/shard_map/all_to_all | solution.py:75
  59.5 4.5 %broadcast_in_dim.5 = bf16[1024,16,128]{2,1,0:T(8,128)(2,1)S(1)} broadcast(bf16[1024,16]{1,0:T(8,128)(2,1)S(1)} %bitcast.55), dimensions={0,1} | broadcast | bytes 4227072 | tf_op jit(solution)/shard_map/broadcast_in_dim | solution.py:8
  69.7 3.5 %all-to-all-done.2 = bf16[8,128,256]{2,1,0:T(8,128)(2,1)} async-done(((bf16[8,128,256]{2,1,0:T(8,128)(2,1)}), bf16[8,128,256]{2,1,0:T(8,128)(2,1)}, u32[]{:S(2)}, u32[]{:S(2)}) %all-to-all-start.2) | async-done | bytes 524320 | tf_op jit(solution)/shard_map/all_to_all | solution.py:75
  73.2 4.1 %all-to-all-start.3 = ((bf16[8,128,256]{2,1,0:T(8,128)(2,1)}), bf16[8,128,256]{2,1,0:T(8,128)(2,1)}, u32[]{:S(2)}, u32[]{:S(2)}) async-start(bf16[8,128,256]{2,1,0:T(8,128)(2,1)} %bitcast.57), calls=%async_computation.3 | async-start | bytes 1048576 | tf_op jit(solution)/shard_map/all_to_all | solution.py:79
  77.4 5.7 %gather_fusion.3 = bf16[1024,256]{1,0:T(8,128)(2,1)} fusion(bf16[1024,256]{1,0:T(8,128)(2,1)} %bitcast.48, s32[1024]{0:T(1024)S(1)} %broadcast_clamp_fusion), kind=kCustom, calls=%fused_computation.3 | custom fusion | bytes 1052672 | tf_op jit(solution)/shard_map/gather | solution.py:54
  83.1 3.9 %fusion.11 = f32[1024,256]{1,0:T(8,128)} fusion(bf16[1024,256]{1,0:T(8,128)(2,1)S(1)} %bitcast.47, bf16[1024,1024]{1,0:T(8,128)(2,1)} %param.16, bf16[1024,2048]{1,0:T(8,128)(2,1)} %bitcast.51), kind=kOutput, calls=%fused_computation.25 | convolution fusion | flops 537919488 | bytes 5767168 | tf_op jit(solution)/shard_map/dot_general | solution.py:16
  87.0 3.7 %all-to-all-done.3 = bf16[8,128,256]{2,1,0:T(8,128)(2,1)} async-done(((bf16[8,128,256]{2,1,0:T(8,128)(2,1)}), bf16[8,128,256]{2,1,0:T(8,128)(2,1)}, u32[]{:S(2)}, u32[]{:S(2)}) %all-to-all-start.3) | async-done | bytes 524320 | tf_op jit(solution)/shard_map/all_to_all | solution.py:79
  90.7 3.7 %all-to-all-start.5 = ((bf16[8,128,256]{2,1,0:T(8,128)(2,1)}), bf16[8,128,256]{2,1,0:T(8,128)(2,1)S(1)}, u32[]{:S(2)}, u32[]{:S(2)}) async-start(bf16[8,128,256]{2,1,0:T(8,128)(2,1)} %bitcast.53), calls=%async_computation.5 | async-start | bytes 1048576 | tf_op jit(solution)/shard_map/all_to_all | solution.py:76
  94.4 3.1 %convolution_add_fusion.2 = f32[1024,256]{1,0:T(8,128)} fusion(f32[1024,256]{1,0:T(8,128)} %fusion.11, bf16[1024,1024]{1,0:T(8,128)(2,1)S(1)} %slice_multiply_fusion, bf16[1024,256]{1,0:T(8,128)(2,1)} %bitcast.10), kind=kOutput, calls=%fused_computation.17 | convolution fusion | flops 537133056 | bytes 4718592 | tf_op jit(solution)/shard_map/dot_general | solution.py:17
  97.5 3.2 %fusion.7 = bf16[1024,256]{1,0:T(8,128)(2,1)} fusion(bf16[256,256]{1,0:T(8,128)(2,1)S(1)} %copy-done.8, f32[1024,256]{1,0:T(8,128)} %convolution_add_fusion.2, bf16[1024,256]{1,0:T(8,128)(2,1)} %bitcast.13, s32[1024]{0:T(1024)S(1)} %bitcast.59, f32[256]{0:T(256)S(1)} %copy-done.9), kind=kOutput, calls=%fused_computation.18 | convolution fusion | flops 673447936 | bytes 2233344 | tf_op jit(solution)/shard_map/dot_general | solution.py:89
  100.7 2.6 convolution_convert_fusion.1
  103.3 4.8 %all-to-all-done.5 = bf16[8,128,256]{2,1,0:T(8,128)(2,1)S(1)} async-done(((bf16[8,128,256]{2,1,0:T(8,128)(2,1)}), bf16[8,128,256]{2,1,0:T(8,128)(2,1)S(1)}, u32[]{:S(2)}, u32[]{:S(2)}) %all-to-all-start.5) | async-done | bytes 524320 | tf_op jit(solution)/shard_map/all_to_all | solution.py:76
  108.2 4.1 %all-to-all-start.6 = ((bf16[8,128,256]{2,1,0:T(8,128)(2,1)}), bf16[8,128,256]{2,1,0:T(8,128)(2,1)}, u32[]{:S(2)}, u32[]{:S(2)}) async-start(bf16[8,128,256]{2,1,0:T(8,128)(2,1)} %bitcast.56), calls=%async_computation.6 | async-start | bytes 1048576 | tf_op jit(solution)/shard_map/all_to_all | solution.py:92
  112.5 3.0 %fusion.10 = f32[1024,256]{1,0:T(8,128)S(1)} fusion(bf16[1024,256]{1,0:T(8,128)(2,1)} %fusion.7, bf16[1024,1024]{1,0:T(8,128)(2,1)} %param.16, bf16[1024,2048]{1,0:T(8,128)(2,1)} %bitcast.52), kind=kOutput, calls=%fused_computation.24 | convolution fusion | flops 537919488 | bytes 5767168 | tf_op jit(solution)/shard_map/dot_general | solution.py:16
  117.3 8.4 %all-to-all-done.6 = bf16[8,128,256]{2,1,0:T(8,128)(2,1)} async-done(((bf16[8,128,256]{2,1,0:T(8,128)(2,1)}), bf16[8,128,256]{2,1,0:T(8,128)(2,1)}, u32[]{:S(2)}, u32[]{:S(2)}) %all-to-all-start.6) | async-done | bytes 524320 | tf_op jit(solution)/shard_map/all_to_all | solution.py:92
  125.7 2.2 fusion.8
  130.1 124.7 %all-reduce.2.cloned.1.call-done = f32[256,256]{1,0:T(8,128)} async-done(((f32[256,256]{1,0:T(8,128)}), f32[256,256]{1,0:T(8,128)}) %all-reduce.2.cloned.1.call-update) | async-done | bytes 262160 | tf_op jit(solution)/shard_map/psum | solution.py:106
  (38 shorter events, 15.0 us)
Async XLA Ops:
  7.2 8.2 %copy-start = (bf16[1024,256]{1,0:T(8,128)(2,1)S(1)}, bf16[1024,256]{1,0:T(8,128)(2,1)}, u32[]{:S(2)}) copy-start(bf16[1024,256]{1,0:T(8,128)(2,1)} %param.11) | copy-start | bytes 1572868
  7.2 17.4 %copy-start.5 = (bf16[1024,256]{1,0:T(8,128)(2,1)S(1)}, bf16[1024,256]{1,0:T(8,128)(2,1)}, u32[]{:S(2)}) copy-start(bf16[1024,256]{1,0:T(8,128)(2,1)} %param.12) | copy-start | bytes 1572868
  7.2 13.9 %all-to-all-start.1 = ((s32[8,1,128]{2,1,0:T(1,128)}), s32[8,1,128]{2,1,0:T(1,128)S(1)}, u32[]{:S(2)}, u32[]{:S(2)}) async-start(s32[8,1,128]{2,1,0:T(1,128)} %bitcast.62), calls=%async_computation.1 | async-start | bytes 8192 | tf_op jit(solution)/shard_map/all_to_all | solution.py:49
  21.1 16.8 %all-to-all-start = ((bf16[8,128,256]{2,1,0:T(8,128)(2,1)}), bf16[8,128,256]{2,1,0:T(8,128)(2,1)S(1)}, u32[]{:S(2)}, u32[]{:S(2)}) async-start(bf16[8,128,256]{2,1,0:T(8,128)(2,1)} %gather_fusion), calls=%async_computation | async-start | bytes 1048576 | tf_op jit(solution)/shard_map/all_to_all | solution.py:69
  37.8 17.5 %all-to-all-start.4 = ((bf16[8,128,256]{2,1,0:T(8,128)(2,1)}), bf16[8,128,256]{2,1,0:T(8,128)(2,1)S(1)}, u32[]{:S(2)}, u32[]{:S(2)}) async-start(bf16[8,128,256]{2,1,0:T(8,128)(2,1)} %gather_fusion.2), calls=%async_computation.4 | async-start | bytes 1048576 | tf_op jit(solution)/shard_map/all_to_all | solution.py:70
  41.5 18.0 %copy-start.7 = (s32[8,16]{1,0:T(8,128)S(1)}, s32[8,16]{1,0:T(8,128)}, u32[]{:S(2)}) copy-start(s32[8,16]{1,0:T(8,128)} %param.15) | copy-start | bytes 1540
  55.3 8.7 %copy-start.1 = (bf16[8,128,256]{2,1,0:T(8,128)(2,1)}, bf16[8,128,256]{2,1,0:T(8,128)(2,1)S(1)}, u32[]{:S(2)}) copy-start(bf16[8,128,256]{2,1,0:T(8,128)(2,1)S(1)} %all-to-all-done.4) | copy-start | bytes 1572868
  55.3 17.9 %all-to-all-start.2 = ((bf16[8,128,256]{2,1,0:T(8,128)(2,1)}), bf16[8,128,256]{2,1,0:T(8,128)(2,1)}, u32[]{:S(2)}, u32[]{:S(2)}) async-start(bf16[8,128,256]{2,1,0:T(8,128)(2,1)} %bitcast.9), calls=%async_computation.2 | async-start | bytes 1048576 | tf_op jit(solution)/shard_map/all_to_all | solution.py:75
  64.0 2.2 copy-start.3
  66.2 1.9 copy-start.2
  73.2 17.5 %all-to-all-start.3 = ((bf16[8,128,256]{2,1,0:T(8,128)(2,1)}), bf16[8,128,256]{2,1,0:T(8,128)(2,1)}, u32[]{:S(2)}, u32[]{:S(2)}) async-start(bf16[8,128,256]{2,1,0:T(8,128)(2,1)} %bitcast.57), calls=%async_computation.3 | async-start | bytes 1048576 | tf_op jit(solution)/shard_map/all_to_all | solution.py:79
  90.7 17.5 %all-to-all-start.5 = ((bf16[8,128,256]{2,1,0:T(8,128)(2,1)}), bf16[8,128,256]{2,1,0:T(8,128)(2,1)S(1)}, u32[]{:S(2)}, u32[]{:S(2)}) async-start(bf16[8,128,256]{2,1,0:T(8,128)(2,1)} %bitcast.53), calls=%async_computation.5 | async-start | bytes 1048576 | tf_op jit(solution)/shard_map/all_to_all | solution.py:76
  94.4 3.1 %copy-start.8 = (bf16[256,256]{1,0:T(8,128)(2,1)S(1)}, bf16[256,256]{1,0:T(8,128)(2,1)}, u32[]{:S(2)}) copy-start(bf16[256,256]{1,0:T(8,128)(2,1)} %param.18) | copy-start | bytes 393220
  94.4 3.1 %copy-start.9 = (f32[256]{0:T(256)S(1)}, f32[256]{0:T(256)}, u32[]{:S(2)}) copy-start(f32[256]{0:T(256)} %param.19) | copy-start | bytes 3076
  108.2 17.5 %all-to-all-start.6 = ((bf16[8,128,256]{2,1,0:T(8,128)(2,1)}), bf16[8,128,256]{2,1,0:T(8,128)(2,1)}, u32[]{:S(2)}, u32[]{:S(2)}) async-start(bf16[8,128,256]{2,1,0:T(8,128)(2,1)} %bitcast.56), calls=%async_computation.6 | async-start | bytes 1048576 | tf_op jit(solution)/shard_map/all_to_all | solution.py:92
  112.3 142.5 %all-reduce.2.cloned.1.call-start = ((), (), s32[]{:S(2)}) async-start(), calls=%async_computation.7 | async-start | bytes 524288 | tf_op jit(solution)/shard_map/psum | solution.py:106
  117.3 10.7 %copy-start.4 = (bf16[1024,256]{1,0:T(8,128)(2,1)S(1)}, bf16[1024,256]{1,0:T(8,128)(2,1)}, u32[]{:S(2)}) copy-start(bf16[1024,256]{1,0:T(8,128)(2,1)} %param.21) | copy-start | bytes 1572868
  125.7 3.3 %copy-start.6 = (bf16[256,256]{1,0:T(8,128)(2,1)S(1)}, bf16[256,256]{1,0:T(8,128)(2,1)}, u32[]{:S(2)}) copy-start(bf16[256,256]{1,0:T(8,128)(2,1)} %param.20) | copy-start | bytes 393220
Sparse Core Ops, SparseCore 0:
  129.1 125.6 all-reduce.1
where the time goes:
time: 264 us; the launch traced here: 263 us
  waiting for transfers between devices  170 us (64%)
  starting transfers between devices  31 us (12%)
  local copies, waits for them, and re-layouts  23.5 us (9%)
  matrix products  23.5 us (9%)
  between operations  14.2 us (5%)
    psum x1, waiting for transfers between devices, body(): gradient = lax.psum(local_grad, ('dev', 'rep'))  125 us
    all_to_all x1, waiting for transfers between devices, body(): lax.all_to_all(arrange(features), 'dev', split_axis=0, concat_axis=0, til...  11.9 us
    gather x2, local copies, waits for them, and re-layouts, fetch_rows(): return values[requests].reshape(peer_count, per_peer, breadth)  10.7 us
    all_to_all x1, waiting for transfers between devices, body(): lax.all_to_all(arrange(history), 'dev', split_axis=0, concat_axis=0, tile...  8.81 us
    all_to_all x1, waiting for transfers between devices, body(): lax.all_to_all(partial_two.astype(jnp.bfloat16).reshape(peer_count, per_p...  8.41 us
    all_to_all x1, starting transfers between devices, body(): lax.all_to_all(pull_rows.reshape(peer_count, per_peer), 'dev', split_axis...  7.45 us
    dot_general x2, matrix products, dense_terms(): summed = jnp.dot(local_tile, owned, preferred_element_type=jnp.float32)  6.92 us
    unnamed x22, local copies, waits for them, and re-layouts  5.58 us
  transfers between devices with their start and end apart: 8, of which 8 were waited for; matrix products, arithmetic and copies ran while one was open for 16% of the time, Pallas kernels for 0%

commit v1 on v0

--- a/solution.py
+++ b/solution.py
@@ -103,7 +103,9 @@
     local_grad = lax.dot_general(
         aggregate_two, cotangent, (((0,), (0,)), ((), ())), preferred_element_type=jnp.float32
     )
-    gradient = lax.psum(local_grad, ("dev", "rep"))
+    gradient = local_grad
+    for j in ("rep", "dev"):
+        gradient = jax.lax.psum(gradient, j)
     return (hidden, output, gradient)
 
 

time: 264 us -> 244 us (0.924)
  waiting for transfers between devices: 170 us -> 150 us
    psum x1 -> x2, waiting for transfers between devices: 125 us -> 105 us  [body(): gradient = jax.lax.psum(gradient, j)]
  transfers between devices with their start and end apart: 8 -> 9, of which waited for: 8 -> 9; matrix products, arithmetic and copies ran while one was open for 16% -> 17% of each run, Pallas kernels for 0% -> 0%
where the time goes in v1:
time: 244 us; the launch traced here: 243 us
  waiting for transfers between devices  150 us (61%)
  starting transfers between devices  30.8 us (13%)
  local copies, waits for them, and re-layouts  23.5 us (10%)
  matrix products  23.5 us (10%)
  between operations  14.2 us (6%)
    psum x2, waiting for transfers between devices, body(): gradient = jax.lax.psum(gradient, j)  105 us
    all_to_all x1, waiting for transfers between devices, body(): lax.all_to_all(arrange(features), 'dev', split_axis=0, concat_axis=0, til...  11.9 us
    gather x2, local copies, waits for them, and re-layouts, fetch_rows(): return values[requests].reshape(peer_count, per_peer, breadth)  10.7 us
    all_to_all x1, waiting for transfers between devices, body(): lax.all_to_all(arrange(history), 'dev', split_axis=0, concat_axis=0, tile...  8.81 us
    all_to_all x1, waiting for transfers between devices, body(): lax.all_to_all(partial_two.astype(jnp.bfloat16).reshape(peer_count, per_p...  8.59 us
    all_to_all x1, starting transfers between devices, body(): lax.all_to_all(pull_rows.reshape(peer_count, per_peer), 'dev', split_axis...  7.45 us
    dot_general x2, matrix products, dense_terms(): summed = jnp.dot(local_tile, owned, preferred_element_type=jnp.float32)  6.91 us
    unnamed x22, local copies, waits for them, and re-layouts  5.58 us
  transfers between devices with their start and end apart: 9, of which 9 were waited for; matrix products, arithmetic and copies ran while one was open for 17% of the time, Pallas kernels for 0%

profile of v1, /device:TPU:0, one launch (start us, length us, event | category | flops | bytes accessed | tf_op | source)
XLA Modules:
  0.0 243.5 jit_solution(10179461771275953720)
XLA Ops:
  7.2 7.5 %all-to-all-start.1 = ((s32[8,1,128]{2,1,0:T(1,128)}), s32[8,1,128]{2,1,0:T(1,128)S(1)}, u32[]{:S(2)}, u32[]{:S(2)}) async-start(s32[8,1,128]{2,1,0:T(1,128)} %bitcast.62), calls=%async_computation.1 | async-start | bytes 8192 | tf_op jit(solution)/shard_map/all_to_all | solution.py:49
  16.8 4.3 %all-to-all-done.1 = s32[8,1,128]{2,1,0:T(1,128)S(1)} async-done(((s32[8,1,128]{2,1,0:T(1,128)}), s32[8,1,128]{2,1,0:T(1,128)S(1)}, u32[]{:S(2)}, u32[]{:S(2)}) %all-to-all-start.1) | async-done | bytes 4128 | tf_op jit(solution)/shard_map/all_to_all | solution.py:49
  21.1 3.5 %all-to-all-start = ((bf16[8,128,256]{2,1,0:T(8,128)(2,1)}), bf16[8,128,256]{2,1,0:T(8,128)(2,1)S(1)}, u32[]{:S(2)}, u32[]{:S(2)}) async-start(bf16[8,128,256]{2,1,0:T(8,128)(2,1)} %gather_fusion), calls=%async_computation | async-start | bytes 1048576 | tf_op jit(solution)/shard_map/all_to_all | solution.py:69
  25.9 11.9 %all-to-all-done = bf16[8,128,256]{2,1,0:T(8,128)(2,1)S(1)} async-done(((bf16[8,128,256]{2,1,0:T(8,128)(2,1)}), bf16[8,128,256]{2,1,0:T(8,128)(2,1)S(1)}, u32[]{:S(2)}, u32[]{:S(2)}) %all-to-all-start) | async-done | bytes 524320 | tf_op jit(solution)/shard_map/all_to_all | solution.py:69
  37.8 3.7 %all-to-all-start.4 = ((bf16[8,128,256]{2,1,0:T(8,128)(2,1)}), bf16[8,128,256]{2,1,0:T(8,128)(2,1)S(1)}, u32[]{:S(2)}, u32[]{:S(2)}) async-start(bf16[8,128,256]{2,1,0:T(8,128)(2,1)} %gather_fusion.2), calls=%async_computation.4 | async-start | bytes 1048576 | tf_op jit(solution)/shard_map/all_to_all | solution.py:70
  41.5 5.0 %gather_fusion.1 = bf16[1024,256]{1,0:T(8,128)(2,1)} fusion(bf16[1024,256]{1,0:T(8,128)(2,1)S(1)} %bitcast.45, s32[1024]{0:T(1024)S(1)} %broadcast_clamp_fusion), kind=kCustom, calls=%fused_computation.1 | custom fusion | bytes 1052672 | tf_op jit(solution)/shard_map/gather | solution.py:54
  46.5 8.8 %all-to-all-done.4 = bf16[8,128,256]{2,1,0:T(8,128)(2,1)S(1)} async-done(((bf16[8,128,256]{2,1,0:T(8,128)(2,1)}), bf16[8,128,256]{2,1,0:T(8,128)(2,1)S(1)}, u32[]{:S(2)}, u32[]{:S(2)}) %all-to-all-start.4) | async-done | bytes 524320 | tf_op jit(solution)/shard_map/all_to_all | solution.py:70
  55.3 4.2 %all-to-all-start.2 = ((bf16[8,128,256]{2,1,0:T(8,128)(2,1)}), bf16[8,128,256]{2,1,0:T(8,128)(2,1)}, u32[]{:S(2)}, u32[]{:S(2)}) async-start(bf16[8,128,256]{2,1,0:T(8,128)(2,1)} %bitcast.9), calls=%async_computation.2 | async-start | bytes 1048576 | tf_op jit(solution)/shard_map/all_to_all | solution.py:75
  59.5 4.5 %broadcast_in_dim.5 = bf16[1024,16,128]{2,1,0:T(8,128)(2,1)S(1)} broadcast(bf16[1024,16]{1,0:T(8,128)(2,1)S(1)} %bitcast.55), dimensions={0,1} | broadcast | bytes 4227072 | tf_op jit(solution)/shard_map/broadcast_in_dim | solution.py:8
  69.7 3.5 %all-to-all-done.2 = bf16[8,128,256]{2,1,0:T(8,128)(2,1)} async-done(((bf16[8,128,256]{2,1,0:T(8,128)(2,1)}), bf16[8,128,256]{2,1,0:T(8,128)(2,1)}, u32[]{:S(2)}, u32[]{:S(2)}) %all-to-all-start.2) | async-done | bytes 524320 | tf_op jit(solution)/shard_map/all_to_all | solution.py:75
  73.2 4.1 %all-to-all-start.3 = ((bf16[8,128,256]{2,1,0:T(8,128)(2,1)}), bf16[8,128,256]{2,1,0:T(8,128)(2,1)}, u32[]{:S(2)}, u32[]{:S(2)}) async-start(bf16[8,128,256]{2,1,0:T(8,128)(2,1)} %bitcast.57), calls=%async_computation.3 | async-start | bytes 1048576 | tf_op jit(solution)/shard_map/all_to_all | solution.py:79
  77.4 5.7 %gather_fusion.3 = bf16[1024,256]{1,0:T(8,128)(2,1)} fusion(bf16[1024,256]{1,0:T(8,128)(2,1)} %bitcast.48, s32[1024]{0:T(1024)S(1)} %broadcast_clamp_fusion), kind=kCustom, calls=%fused_computation.3 | custom fusion | bytes 1052672 | tf_op jit(solution)/shard_map/gather | solution.py:54
  83.1 3.9 %fusion.11 = f32[1024,256]{1,0:T(8,128)} fusion(bf16[1024,256]{1,0:T(8,128)(2,1)S(1)} %bitcast.47, bf16[1024,1024]{1,0:T(8,128)(2,1)} %param.16, bf16[1024,2048]{1,0:T(8,128)(2,1)} %bitcast.51), kind=kOutput, calls=%fused_computation.25 | convolution fusion | flops 537919488 | bytes 5767168 | tf_op jit(solution)/shard_map/dot_general | solution.py:16
  87.0 3.7 %all-to-all-done.3 = bf16[8,128,256]{2,1,0:T(8,128)(2,1)} async-done(((bf16[8,128,256]{2,1,0:T(8,128)(2,1)}), bf16[8,128,256]{2,1,0:T(8,128)(2,1)}, u32[]{:S(2)}, u32[]{:S(2)}) %all-to-all-start.3) | async-done | bytes 524320 | tf_op jit(solution)/shard_map/all_to_all | solution.py:79
  90.7 3.7 %all-to-all-start.5 = ((bf16[8,128,256]{2,1,0:T(8,128)(2,1)}), bf16[8,128,256]{2,1,0:T(8,128)(2,1)S(1)}, u32[]{:S(2)}, u32[]{:S(2)}) async-start(bf16[8,128,256]{2,1,0:T(8,128)(2,1)} %bitcast.53), calls=%async_computation.5 | async-start | bytes 1048576 | tf_op jit(solution)/shard_map/all_to_all | solution.py:76
  94.4 3.1 %convolution_add_fusion.2 = f32[1024,256]{1,0:T(8,128)} fusion(f32[1024,256]{1,0:T(8,128)} %fusion.11, bf16[1024,1024]{1,0:T(8,128)(2,1)S(1)} %slice_multiply_fusion, bf16[1024,256]{1,0:T(8,128)(2,1)} %bitcast.10), kind=kOutput, calls=%fused_computation.17 | convolution fusion | flops 537133056 | bytes 4718592 | tf_op jit(solution)/shard_map/dot_general | solution.py:17
  97.5 3.2 %fusion.7 = bf16[1024,256]{1,0:T(8,128)(2,1)} fusion(bf16[256,256]{1,0:T(8,128)(2,1)S(1)} %copy-done.8, f32[1024,256]{1,0:T(8,128)} %convolution_add_fusion.2, bf16[1024,256]{1,0:T(8,128)(2,1)} %bitcast.13, s32[1024]{0:T(1024)S(1)} %bitcast.59, f32[256]{0:T(256)S(1)} %copy-done.9), kind=kOutput, calls=%fused_computation.18 | convolution fusion | flops 673447936 | bytes 2233344 | tf_op jit(solution)/shard_map/dot_general | solution.py:89
  100.7 2.6 %convolution_convert_fusion.1 = bf16[1024,256]{1,0:T(8,128)(2,1)} fusion(bf16[1024,1024]{1,0:T(8,128)(2,1)S(1)} %slice_multiply_fusion, bf16[1024,256]{1,0:T(8,128)(2,1)} %fusion.7), kind=kOutput, calls=%fused_computation.22 | convolution fusion | flops 537133056 | bytes 3145728 | tf_op jit(solution)/shard_map/dot_general | solution.py:18
  103.3 4.8 %all-to-all-done.5 = bf16[8,128,256]{2,1,0:T(8,128)(2,1)S(1)} async-done(((bf16[8,128,256]{2,1,0:T(8,128)(2,1)}), bf16[8,128,256]{2,1,0:T(8,128)(2,1)S(1)}, u32[]{:S(2)}, u32[]{:S(2)}) %all-to-all-start.5) | async-done | bytes 524320 | tf_op jit(solution)/shard_map/all_to_all | solution.py:76
  108.2 4.1 %all-to-all-start.6 = ((bf16[8,128,256]{2,1,0:T(8,128)(2,1)}), bf16[8,128,256]{2,1,0:T(8,128)(2,1)}, u32[]{:S(2)}, u32[]{:S(2)}) async-start(bf16[8,128,256]{2,1,0:T(8,128)(2,1)} %bitcast.56), calls=%async_computation.6 | async-start | bytes 1048576 | tf_op jit(solution)/shard_map/all_to_all | solution.py:92
  112.4 3.0 %fusion.10 = f32[1024,256]{1,0:T(8,128)S(1)} fusion(bf16[1024,256]{1,0:T(8,128)(2,1)} %fusion.7, bf16[1024,1024]{1,0:T(8,128)(2,1)} %param.16, bf16[1024,2048]{1,0:T(8,128)(2,1)} %bitcast.52), kind=kOutput, calls=%fused_computation.24 | convolution fusion | flops 537919488 | bytes 5767168 | tf_op jit(solution)/shard_map/dot_general | solution.py:16
  117.1 8.6 %all-to-all-done.6 = bf16[8,128,256]{2,1,0:T(8,128)(2,1)} async-done(((bf16[8,128,256]{2,1,0:T(8,128)(2,1)}), bf16[8,128,256]{2,1,0:T(8,128)(2,1)}, u32[]{:S(2)}, u32[]{:S(2)}) %all-to-all-start.6) | async-done | bytes 524320 | tf_op jit(solution)/shard_map/all_to_all | solution.py:92
  129.1 31.5 %all-reduce.3.cloned.1.call-done = f32[256,256]{1,0:T(8,128)} async-done(((f32[256,256]{1,0:T(8,128)}), f32[256,256]{1,0:T(8,128)}) %all-reduce.3.cloned.1.call-update) | async-done | bytes 262160 | tf_op jit(solution)/shard_map/psum | solution.py:108
  161.7 73.3 %all-reduce.5.cloned.1.call-done = f32[256,256]{1,0:T(8,128)} async-done(((f32[256,256]{1,0:T(8,128)}), f32[256,256]{1,0:T(8,128)}) %all-reduce.5.cloned.1.call-update) | async-done | bytes 262160 | tf_op jit(solution)/shard_map/psum | solution.py:108
  (41 shorter events, 17.1 us)
Async XLA Ops:
  7.2 8.2 %copy-start = (bf16[1024,256]{1,0:T(8,128)(2,1)S(1)}, bf16[1024,256]{1,0:T(8,128)(2,1)}, u32[]{:S(2)}) copy-start(bf16[1024,256]{1,0:T(8,128)(2,1)} %param.11) | copy-start | bytes 1572868
  7.2 17.4 %copy-start.5 = (bf16[1024,256]{1,0:T(8,128)(2,1)S(1)}, bf16[1024,256]{1,0:T(8,128)(2,1)}, u32[]{:S(2)}) copy-start(bf16[1024,256]{1,0:T(8,128)(2,1)} %param.12) | copy-start | bytes 1572868
  7.2 13.9 %all-to-all-start.1 = ((s32[8,1,128]{2,1,0:T(1,128)}), s32[8,1,128]{2,1,0:T(1,128)S(1)}, u32[]{:S(2)}, u32[]{:S(2)}) async-start(s32[8,1,128]{2,1,0:T(1,128)} %bitcast.62), calls=%async_computation.1 | async-start | bytes 8192 | tf_op jit(solution)/shard_map/all_to_all | solution.py:49
  21.1 16.8 %all-to-all-start = ((bf16[8,128,256]{2,1,0:T(8,128)(2,1)}), bf16[8,128,256]{2,1,0:T(8,128)(2,1)S(1)}, u32[]{:S(2)}, u32[]{:S(2)}) async-start(bf16[8,128,256]{2,1,0:T(8,128)(2,1)} %gather_fusion), calls=%async_computation | async-start | bytes 1048576 | tf_op jit(solution)/shard_map/all_to_all | solution.py:69
  37.8 17.5 %all-to-all-start.4 = ((bf16[8,128,256]{2,1,0:T(8,128)(2,1)}), bf16[8,128,256]{2,1,0:T(8,128)(2,1)S(1)}, u32[]{:S(2)}, u32[]{:S(2)}) async-start(bf16[8,128,256]{2,1,0:T(8,128)(2,1)} %gather_fusion.2), calls=%async_computation.4 | async-start | bytes 1048576 | tf_op jit(solution)/shard_map/all_to_all | solution.py:70
  41.5 18.0 %copy-start.7 = (s32[8,16]{1,0:T(8,128)S(1)}, s32[8,16]{1,0:T(8,128)}, u32[]{:S(2)}) copy-start(s32[8,16]{1,0:T(8,128)} %param.15) | copy-start | bytes 1540
  55.3 8.7 %copy-start.1 = (bf16[8,128,256]{2,1,0:T(8,128)(2,1)}, bf16[8,128,256]{2,1,0:T(8,128)(2,1)S(1)}, u32[]{:S(2)}) copy-start(bf16[8,128,256]{2,1,0:T(8,128)(2,1)S(1)} %all-to-all-done.4) | copy-start | bytes 1572868
  55.3 17.9 %all-to-all-start.2 = ((bf16[8,128,256]{2,1,0:T(8,128)(2,1)}), bf16[8,128,256]{2,1,0:T(8,128)(2,1)}, u32[]{:S(2)}, u32[]{:S(2)}) async-start(bf16[8,128,256]{2,1,0:T(8,128)(2,1)} %bitcast.9), calls=%async_computation.2 | async-start | bytes 1048576 | tf_op jit(solution)/shard_map/all_to_all | solution.py:75
  64.0 2.2 copy-start.3
  66.2 1.9 copy-start.2
  73.2 17.5 %all-to-all-start.3 = ((bf16[8,128,256]{2,1,0:T(8,128)(2,1)}), bf16[8,128,256]{2,1,0:T(8,128)(2,1)}, u32[]{:S(2)}, u32[]{:S(2)}) async-start(bf16[8,128,256]{2,1,0:T(8,128)(2,1)} %bitcast.57), calls=%async_computation.3 | async-start | bytes 1048576 | tf_op jit(solution)/shard_map/all_to_all | solution.py:79
  90.7 17.5 %all-to-all-start.5 = ((bf16[8,128,256]{2,1,0:T(8,128)(2,1)}), bf16[8,128,256]{2,1,0:T(8,128)(2,1)S(1)}, u32[]{:S(2)}, u32[]{:S(2)}) async-start(bf16[8,128,256]{2,1,0:T(8,128)(2,1)} %bitcast.53), calls=%async_computation.5 | async-start | bytes 1048576 | tf_op jit(solution)/shard_map/all_to_all | solution.py:76
  94.4 3.1 %copy-start.8 = (bf16[256,256]{1,0:T(8,128)(2,1)S(1)}, bf16[256,256]{1,0:T(8,128)(2,1)}, u32[]{:S(2)}) copy-start(bf16[256,256]{1,0:T(8,128)(2,1)} %param.18) | copy-start | bytes 393220
  94.4 3.1 %copy-start.9 = (f32[256]{0:T(256)S(1)}, f32[256]{0:T(256)}, u32[]{:S(2)}) copy-start(f32[256]{0:T(256)} %param.19) | copy-start | bytes 3076
  108.2 17.5 %all-to-all-start.6 = ((bf16[8,128,256]{2,1,0:T(8,128)(2,1)}), bf16[8,128,256]{2,1,0:T(8,128)(2,1)}, u32[]{:S(2)}, u32[]{:S(2)}) async-start(bf16[8,128,256]{2,1,0:T(8,128)(2,1)} %bitcast.56), calls=%async_computation.6 | async-start | bytes 1048576 | tf_op jit(solution)/shard_map/all_to_all | solution.py:92
  112.3 48.2 %all-reduce.3.cloned.1.call-start = ((), (), s32[]{:S(2)}) async-start(), calls=%async_computation.7 | async-start | bytes 524288 | tf_op jit(solution)/shard_map/psum | solution.py:108
  117.1 10.8 %copy-start.4 = (bf16[1024,256]{1,0:T(8,128)(2,1)S(1)}, bf16[1024,256]{1,0:T(8,128)(2,1)}, u32[]{:S(2)}) copy-start(bf16[1024,256]{1,0:T(8,128)(2,1)} %param.21) | copy-start | bytes 1572868
  125.7 34.9 %copy-start.6 = (bf16[256,256]{1,0:T(8,128)(2,1)S(1)}, bf16[256,256]{1,0:T(8,128)(2,1)}, u32[]{:S(2)}) copy-start(bf16[256,256]{1,0:T(8,128)(2,1)} %param.20) | copy-start | bytes 393220
  129.0 105.9 %all-reduce.5.cloned.1.call-start = ((), (), s32[]{:S(2)}) async-start(), calls=%async_computation.8 | async-start | bytes 524288 | tf_op jit(solution)/shard_map/psum | solution.py:108
Sparse Core Ops, SparseCore 0:
  129.1 31.3 all-reduce.2
  163.9 71.0 all-reduce.4
